TPU v7x, 32 devices: a whole 2x2x4 slice. The times are simulated.
32 devices in a mesh: head: 4 (over y, core), blk: 8 (over z, x).
Axes of the slice: x: 2, y: 2, z: 4, core: 2. Of those that a mesh axis runs over, the one named last changes fastest.
Arguments:
- block_input: bfloat16 [4096, 1024], P(('head', 'blk')), may hold values from -6 to 6
- span_order: int32 [32], replicated, may hold values from 0 to 31, each once
- norm1_gain: bfloat16 [1024], P(('head', 'blk')), may hold values from 0.099609375 to 1.8984375
- w_query: bfloat16 [1024, 1024], P(('head', 'blk')), may hold values from -0.1875 to 0.1875
- key_weight: bfloat16 [1024, 512], P(('head', 'blk')), may hold values from -0.1875 to 0.1875
- value_weight: bfloat16 [1024, 512], P(('head', 'blk')), may hold values from -0.1875 to 0.1875
- qk_gain: float32 [2, 64], replicated, may hold values from 0.5 to 3, as said below
- w_out: bfloat16 [1024, 1024], P(('head', 'blk')), may hold values from -6 to 6
- norm2_gain: bfloat16 [1024], P(('head', 'blk')), may hold values from 0.099609375 to 1.8984375
- w_gate: bfloat16 [1024, 4608], P(('head', 'blk')), may hold values from -0.1875 to 0.1875
- w_up: bfloat16 [1024, 4608], P(('head', 'blk')), may hold values from -0.1875 to 0.1875
- w_down: bfloat16 [4608, 1024], P(('head', 'blk')), may hold values from -0.09375 to 0.09375
- out_grad: bfloat16 [4096, 1024], P(('head', 'blk')), may hold values from -6 to 6
Outputs:
- block_output: bfloat16 [4096, 1024], P(('head', 'blk'))
- input_grad: bfloat16 [4096, 1024], P(('head', 'blk'))
- norm1_grad: float32 [1024], P(('head', 'blk'))
- query_grad: float32 [1024, 1024], P(('head', 'blk'))
- key_grad: float32 [1024, 512], P(('head', 'blk'))
- value_grad: float32 [1024, 512], P(('head', 'blk'))
- qk_gain_grad: float32 [2, 64], replicated
- out_proj_grad: float32 [1024, 1024], P(('head', 'blk'))
- norm2_grad: float32 [1024], P(('head', 'blk'))
- gate_grad: float32 [1024, 4608], P(('head', 'blk'))
- up_grad: float32 [1024, 4608], P(('head', 'blk'))
- down_grad: float32 [4608, 1024], P(('head', 'blk'))
Inputs may be any that keep to these rules, and one draw needn't show every extreme that they name: Storage span c of 128 rows holds the sequence positions from span_order[c] * 128 on; every span place occurs once. `qk_gain`: positive gains.
All inputs are finite; a program needn't handle non-finite values.
Results may differ from a plain program's by a relative error of at most 0.02.
The roundings to bfloat16 on the way count: a program that leaves them out, or rounds other values in their place, can miss the bound.
Values may be sent and summed in bfloat16 or wider, within the bound.
A program may use at most 512 MiB of HBM per device.

v0:
```python
import math
import jax
import jax.numpy as jnp
from jax import lax
from jax.sharding import PartitionSpec as P

EPS = 1e-05
THETA = 1000000.0
NEG = -1e30


def rms_norm(values, gain_vec):
    inverse = lax.rsqrt(jnp.mean(values * values, axis=-1, keepdims=True) + EPS)
    return values * inverse * gain_vec


def rotate(field_in, where_at):
    half_size = field_in.shape[-1] // 2
    frequency = jnp.exp(
        jnp.arange(half_size, dtype=jnp.float32)
        * jnp.float32(-2.0 * math.log(THETA) / field_in.shape[-1])
    )
    angles = where_at.astype(jnp.float32)[:, None] * frequency[None, :]
    cosine = jnp.cos(angles)[:, None, :]
    sine_part = jnp.sin(angles)[:, None, :]
    first_half = field_in[..., :half_size]
    second_half = field_in[..., half_size:]
    return jnp.concatenate(
        [
            first_half * cosine - second_half * sine_part,
            second_half * cosine + first_half * sine_part,
        ],
        axis=-1,
    )


def head_map(raw_rows, gain_vec, where_at):
    row_count = raw_rows.shape[0]
    shaped = raw_rows.reshape(row_count, -1, gain_vec.shape[0])
    return rotate(rms_norm(shaped, gain_vec), where_at).reshape(row_count, -1)


def lookup(span_ids, order_table):
    matches = span_ids[:, None] == jnp.arange(order_table.shape[0], dtype=jnp.int32)[None, :]
    return jnp.sum(jnp.where(matches, order_table[None, :], 0), axis=1)


def positions(row_ids, tok_rows, blocks, group_rows, order_table):
    span_ids = row_ids % group_rows // tok_rows * blocks + row_ids // group_rows
    return lookup(span_ids, order_table) * tok_rows + row_ids % tok_rows


def local(
    block_input,
    span_order,
    norm1_gain,
    w_query,
    key_weight,
    value_weight,
    qk_gain,
    w_out,
    norm2_gain,
    w_gate,
    w_up,
    w_down,
    out_grad,
):
    blocks = lax.axis_size("blk")
    groups = lax.axis_size("head")
    tok_rows = block_input.shape[0]
    group_rows = groups * tok_rows
    head_size = qk_gain.shape[1]
    kv_total = key_weight.shape[1] // head_size
    kv_local = kv_total // groups
    share_count = w_query.shape[1] // key_weight.shape[1]
    score_scale = float(head_size) ** (-0.5)
    blk_index = lax.axis_index("blk")
    head_index = lax.axis_index("head")
    own_rows = (
        blk_index * group_rows + head_index * tok_rows + jnp.arange(tok_rows, dtype=jnp.int32)
    )
    tok_where = positions(own_rows, tok_rows, blocks, group_rows, span_order)
    query_where = positions(
        blk_index * group_rows + jnp.arange(group_rows, dtype=jnp.int32),
        tok_rows,
        blocks,
        group_rows,
        span_order,
    )
    gathered = (
        lax.all_gather(norm1_gain, ("head", "blk"), axis=0, tiled=True),
        lax.all_gather(w_query, ("head", "blk"), axis=0, tiled=True),
        lax.all_gather(key_weight, ("head", "blk"), axis=0, tiled=True),
        lax.all_gather(value_weight, ("head", "blk"), axis=0, tiled=True),
        lax.all_gather(w_out, ("head", "blk"), axis=0, tiled=True),
        lax.all_gather(norm2_gain, ("head", "blk"), axis=0, tiled=True),
        lax.all_gather(w_gate, ("head", "blk"), axis=0, tiled=True),
        lax.all_gather(w_up, ("head", "blk"), axis=0, tiled=True),
        lax.all_gather(w_down, ("head", "blk"), axis=0, tiled=True),
    )
    (
        gain_one,
        query_full,
        key_full,
        value_full,
        out_full,
        gain_two,
        gate_full,
        up_full,
        down_full,
    ) = gathered
    gain_one = gain_one.astype(jnp.float32)
    gain_two = gain_two.astype(jnp.float32)
    in_flat = block_input.astype(jnp.float32)
    normed = rms_norm(in_flat, gain_one).astype(jnp.bfloat16)
    q_raw = jnp.dot(normed, query_full, preferred_element_type=jnp.float32)
    k_raw = jnp.dot(normed, key_full, preferred_element_type=jnp.float32)
    v_raw = jnp.dot(normed, value_full, preferred_element_type=jnp.float32)

    def query_map(raw_rows, gain_vec):
        return head_map(raw_rows, gain_vec, tok_where)

    queries = query_map(q_raw, qk_gain[0]).astype(jnp.bfloat16)
    keys = query_map(k_raw, qk_gain[1]).astype(jnp.bfloat16)
    values = v_raw.astype(jnp.bfloat16)
    q_heads, k_heads, v_heads = (
        lax.all_to_all(queries, "head", split_axis=1, concat_axis=0, tiled=True),
        lax.all_to_all(keys, "head", split_axis=1, concat_axis=0, tiled=True),
        lax.all_to_all(values, "head", split_axis=1, concat_axis=0, tiled=True),
    )
    q_four = q_heads.reshape(group_rows, kv_local, share_count, head_size)

    def key_where(row_count):
        return positions(
            jnp.arange(row_count, dtype=jnp.int32), tok_rows, blocks, group_rows, span_order
        )

    start_state = (
        jnp.full((kv_local, share_count, group_rows), NEG, jnp.float32),
        jnp.zeros((kv_local, share_count, group_rows), jnp.float32),
        jnp.zeros((group_rows, kv_local, share_count, head_size), jnp.float32),
    )
    key_piece = lax.all_gather(k_heads, "blk", axis=0, tiled=True)
    value_piece = lax.all_gather(v_heads, "blk", axis=0, tiled=True)
    row_count = key_piece.shape[0]
    key_three = key_piece.reshape(row_count, kv_local, head_size)
    value_three = value_piece.reshape(row_count, kv_local, head_size)
    causal = key_where(row_count)[None, :] <= query_where[:, None]

    def update(held_state):
        row_max, row_sum, accumulated = held_state
        scores = (
            jnp.einsum("qkgd,nkd->kgqn", q_four, key_three, preferred_element_type=jnp.float32)
            * score_scale
        )
        scores = jnp.where(causal, scores, NEG)
        new_max = jnp.maximum(row_max, jnp.max(scores, axis=-1))
        weights = jnp.where(causal, jnp.exp(scores - new_max[..., None]), 0.0)
        row_sum = jnp.sum(weights, axis=-1)
        value_part = jnp.einsum(
            "kgqn,nkd->qkgd",
            weights.astype(jnp.bfloat16),
            value_three,
            preferred_element_type=jnp.float32,
        )
        accumulated = value_part
        return (new_max, row_sum, accumulated)

    row_max, row_sum, accumulated = update(start_state)
    attended_heads = (accumulated / row_sum.transpose(2, 0, 1)[..., None]).astype(jnp.bfloat16)
    log_total = row_max + jnp.log(row_sum)
    attended = lax.all_to_all(
        attended_heads.reshape(group_rows, -1), "head", split_axis=0, concat_axis=1, tiled=True
    )
    middle = in_flat + jnp.dot(attended, out_full, preferred_element_type=jnp.float32)
    normed2 = rms_norm(middle, gain_two).astype(jnp.bfloat16)
    gate_rows = jnp.dot(normed2, gate_full, preferred_element_type=jnp.float32)
    up_rows = jnp.dot(normed2, up_full, preferred_element_type=jnp.float32)
    hidden = (jax.nn.silu(gate_rows) * up_rows).astype(jnp.bfloat16)
    block_output = (middle + jnp.dot(hidden, down_full, preferred_element_type=jnp.float32)).astype(
        jnp.bfloat16
    )
    gathered = (
        lax.all_gather(norm1_gain, ("head", "blk"), axis=0, tiled=True),
        lax.all_gather(w_query, ("head", "blk"), axis=0, tiled=True),
        lax.all_gather(key_weight, ("head", "blk"), axis=0, tiled=True),
        lax.all_gather(value_weight, ("head", "blk"), axis=0, tiled=True),
        lax.all_gather(w_out, ("head", "blk"), axis=0, tiled=True),
        lax.all_gather(norm2_gain, ("head", "blk"), axis=0, tiled=True),
        lax.all_gather(w_gate, ("head", "blk"), axis=0, tiled=True),
        lax.all_gather(w_up, ("head", "blk"), axis=0, tiled=True),
        lax.all_gather(w_down, ("head", "blk"), axis=0, tiled=True),
    )
    (
        gain_one,
        query_full,
        key_full,
        value_full,
        out_full,
        gain_two,
        gate_full,
        up_full,
        down_full,
    ) = gathered
    gain_one = gain_one.astype(jnp.float32)
    gain_two = gain_two.astype(jnp.float32)
    dhidden = jnp.dot(out_grad, down_full.T, preferred_element_type=jnp.float32)
    down_grad = jnp.dot(hidden.T, out_grad, preferred_element_type=jnp.float32)
    _, gate_back = jax.vjp(lambda gate_in, up_in: jax.nn.silu(gate_in) * up_in, gate_rows, up_rows)
    dgate, dup = gate_back(dhidden)
    dgate = dgate.astype(jnp.bfloat16)
    dup = dup.astype(jnp.bfloat16)
    dnormed2 = jnp.dot(dgate, gate_full.T, preferred_element_type=jnp.float32) + jnp.dot(
        dup, up_full.T, preferred_element_type=jnp.float32
    )
    gate_grad = jnp.dot(normed2.T, dgate, preferred_element_type=jnp.float32)
    up_grad = jnp.dot(normed2.T, dup, preferred_element_type=jnp.float32)
    _, norm2_back = jax.vjp(rms_norm, middle, gain_two)
    dmiddle_norm, norm2_grad = norm2_back(dnormed2)
    dmiddle = out_grad.astype(jnp.float32) + dmiddle_norm
    dmiddle_b = dmiddle.astype(jnp.bfloat16)
    out_proj_grad = jnp.dot(attended.T, dmiddle_b, preferred_element_type=jnp.float32)
    dattended = jnp.dot(dmiddle_b, out_full.T, preferred_element_type=jnp.float32).astype(
        jnp.bfloat16
    )
    grad_heads = lax.all_to_all(dattended, "head", split_axis=1, concat_axis=0, tiled=True)
    grad_four = grad_heads.reshape(group_rows, kv_local, share_count, head_size)
    delta_rows = jnp.sum(
        grad_four.astype(jnp.float32) * attended_heads.astype(jnp.float32), axis=-1
    ).transpose(1, 2, 0)
    back_state = (
        jnp.zeros((group_rows, kv_local, share_count, head_size), jnp.float32),
        jnp.zeros((blocks * group_rows, kv_local * head_size), jnp.float32),
        jnp.zeros((blocks * group_rows, kv_local * head_size), jnp.float32),
    )
    key_piece = lax.all_gather(k_heads, "blk", axis=0, tiled=True)
    value_piece = lax.all_gather(v_heads, "blk", axis=0, tiled=True)
    row_count = key_piece.shape[0]
    collect_key_three = key_piece.reshape(row_count, kv_local, head_size)
    collect_value_three = value_piece.reshape(row_count, kv_local, head_size)
    collect_causal = key_where(row_count)[None, :] <= query_where[:, None]

    def update(held_state):
        scores = (
            jnp.einsum(
                "qkgd,nkd->kgqn", q_four, collect_key_three, preferred_element_type=jnp.float32
            )
            * score_scale
        )
        scores = jnp.where(collect_causal, scores, NEG)
        prob_rows = jnp.where(collect_causal, jnp.exp(scores - log_total[..., None]), 0.0)
        value_part = jnp.einsum(
            "kgqn,qkgd->nkd",
            prob_rows.astype(jnp.bfloat16),
            grad_four,
            preferred_element_type=jnp.float32,
        )
        dprob = jnp.einsum(
            "qkgd,nkd->kgqn", grad_four, collect_value_three, preferred_element_type=jnp.float32
        )
        dscore = (prob_rows * (dprob - delta_rows[..., None])).astype(jnp.bfloat16)
        query_acc = (
            jnp.einsum(
                "kgqn,nkd->qkgd", dscore, collect_key_three, preferred_element_type=jnp.float32
            )
            * score_scale
        )
        key_part = (
            jnp.einsum("kgqn,qkgd->nkd", dscore, q_four, preferred_element_type=jnp.float32)
            * score_scale
        )
        key_acc = key_part.reshape(row_count, -1)
        value_acc = value_part.reshape(row_count, -1)
        return (query_acc, key_acc, value_acc)

    query_acc, key_acc, value_acc = update(back_state)
    key_sums, value_sums = (
        lax.psum_scatter(
            key_acc.astype(jnp.bfloat16), "blk", scatter_dimension=0, tiled=True
        ).astype(jnp.float32),
        lax.psum_scatter(
            value_acc.astype(jnp.bfloat16), "blk", scatter_dimension=0, tiled=True
        ).astype(jnp.float32),
    )
    dqueries, dkeys, dvalues = (
        lax.all_to_all(
            query_acc.reshape(group_rows, -1).astype(jnp.bfloat16),
            "head",
            split_axis=0,
            concat_axis=1,
            tiled=True,
        ),
        lax.all_to_all(
            key_sums.astype(jnp.bfloat16), "head", split_axis=0, concat_axis=1, tiled=True
        ),
        lax.all_to_all(
            value_sums.astype(jnp.bfloat16), "head", split_axis=0, concat_axis=1, tiled=True
        ),
    )
    _, query_back = jax.vjp(query_map, q_raw, qk_gain[0])
    dq_raw, qgain_grad = query_back(dqueries.astype(jnp.float32))
    _, key_back = jax.vjp(query_map, k_raw, qk_gain[1])
    dk_raw, kgain_grad = key_back(dkeys.astype(jnp.float32))
    dq_raw = dq_raw.astype(jnp.bfloat16)
    dk_raw = dk_raw.astype(jnp.bfloat16)
    dnormed = jnp.dot(dq_raw, query_full.T, preferred_element_type=jnp.float32)
    dnormed = dnormed + jnp.dot(dk_raw, key_full.T, preferred_element_type=jnp.float32)
    dnormed = dnormed + jnp.dot(dvalues, value_full.T, preferred_element_type=jnp.float32)
    query_grad = jnp.dot(normed.T, dq_raw, preferred_element_type=jnp.float32)
    key_grad = jnp.dot(normed.T, dk_raw, preferred_element_type=jnp.float32)
    value_grad = jnp.dot(normed.T, dvalues, preferred_element_type=jnp.float32)
    _, norm1_back = jax.vjp(rms_norm, in_flat, gain_one)
    dinput_norm, norm1_grad = norm1_back(dnormed)
    input_grad = (dmiddle + dinput_norm).astype(jnp.bfloat16)
    summed = (
        lax.psum_scatter(norm1_grad, ("head", "blk"), scatter_dimension=0, tiled=True),
        lax.psum_scatter(query_grad, ("head", "blk"), scatter_dimension=0, tiled=True),
        lax.psum_scatter(key_grad, ("head", "blk"), scatter_dimension=0, tiled=True),
        lax.psum_scatter(value_grad, ("head", "blk"), scatter_dimension=0, tiled=True),
        lax.psum_scatter(out_proj_grad, ("head", "blk"), scatter_dimension=0, tiled=True),
        lax.psum_scatter(norm2_grad, ("head", "blk"), scatter_dimension=0, tiled=True),
        lax.psum_scatter(gate_grad, ("head", "blk"), scatter_dimension=0, tiled=True),
        lax.psum_scatter(up_grad, ("head", "blk"), scatter_dimension=0, tiled=True),
        lax.psum_scatter(down_grad, ("head", "blk"), scatter_dimension=0, tiled=True),
    )
    qk_gain_grad = lax.psum(jnp.stack([qgain_grad, kgain_grad]), ("head", "blk"))
    return (
        block_output,
        input_grad,
        summed[0],
        summed[1],
        summed[2],
        summed[3],
        qk_gain_grad,
        summed[4],
        summed[5],
        summed[6],
        summed[7],
        summed[8],
    )


def solution(mesh):
    in_specs = (
        P(("head", "blk"), None),
        P(),
        P(("head", "blk")),
        P(("head", "blk"), None),
        P(("head", "blk"), None),
        P(("head", "blk"), None),
        P(),
        P(("head", "blk"), None),
        P(("head", "blk")),
        P(("head", "blk"), None),
        P(("head", "blk"), None),
        P(("head", "blk"), None),
        P(("head", "blk"), None),
    )
    out_specs = (
        P(("head", "blk"), None),
        P(("head", "blk"), None),
        P(("head", "blk")),
        P(("head", "blk"), None),
        P(("head", "blk"), None),
        P(("head", "blk"), None),
        P(),
        P(("head", "blk"), None),
        P(("head", "blk")),
        P(("head", "blk"), None),
        P(("head", "blk"), None),
        P(("head", "blk"), None),
    )
    return jax.shard_map(local, mesh=mesh, in_specs=in_specs, out_specs=out_specs, check_vma=False)
```

profile of v0, /device:TPU:0, one launch (start us, length us, event | category | flops | bytes accessed | tf_op | source)
XLA Modules:
  0.0 1968.1 jit_solution(9084363389160186047)
XLA Ops:
  11.1 42.0 %all-reduce.9 = (bf16[1024]{0:T(1024)(128)(2,1)S(1)}, bf16[1024]{0:T(1024)(128)(2,1)S(1)}) all-reduce(bf16[1024]{0:T(1024)(128)(2,1)S(1)} %dynamic-update-slice, bf16[1024]{0:T(1024)(128)(2,1)S(1)} %dynamic-update-slice.1), channel_id=1, replica_groups=mesh['head'=4,'blk'=8] {'head','blk'}, use_global_device_ids=true, to_apply=%add.4 | all-reduce | flops 2048 | bytes 8192
  54.9 12.6 all-gather.10.cloned.1.call-done
  79.5 43.9 %all-gather.14.cloned.1.call-done = bf16[1024,512]{1,0:T(8,128)(2,1)} async-done(((bf16[32,512]{1,0:T(8,128)(2,1)}), bf16[1024,512]{1,0:T(8,128)(2,1)}) %all-gather.14.cloned.1.call-update) | async-done | bytes 1048592 | tf_op jit(solution)/shard_map/all_gather | solution.py:93
  138.5 43.2 %all-gather.18.cloned.1.call-done = bf16[1024,1024]{1,0:T(8,128)(2,1)} async-done(((bf16[32,1024]{1,0:T(8,128)(2,1)}), bf16[1024,1024]{1,0:T(8,128)(2,1)}) %all-gather.18.cloned.1.call-update) | async-done | bytes 2097168 | tf_op jit(solution)/shard_map/all_gather | solution.py:92
  191.4 32.0 %all-gather.12.cloned.1.call-done = bf16[4096,128]{1,0:T(8,128)(2,1)} async-done(((bf16[512,128]{1,0:T(8,128)(2,1)}), bf16[4096,128]{1,0:T(8,128)(2,1)}) %all-gather.12.cloned.1.call-update) | async-done | bytes 1048592 | tf_op jit(solution)/shard_map/all_gather | solution.py:144
  225.8 39.3 %all-gather.16.cloned.1.call-done = bf16[4096,128]{1,0:T(8,128)(2,1)} async-done(((bf16[512,128]{1,0:T(8,128)(2,1)}), bf16[4096,128]{1,0:T(8,128)(2,1)}) %all-gather.16.cloned.1.call-update) | async-done | bytes 1048592 | tf_op jit(solution)/shard_map/all_gather | solution.py:143
  266.9 15.1 fusion.5
  282.1 15.2 fusion.2
  297.3 15.4 fusion.34
  325.9 80.5 %all-gather.24.cloned.1.call-done = bf16[1024,4608]{1,0:T(8,128)(2,1)} async-done(((bf16[32,4608]{1,0:T(8,128)(2,1)}), bf16[1024,4608]{1,0:T(8,128)(2,1)}) %all-gather.24.cloned.1.call-update) | async-done | bytes 9437200 | tf_op jit(solution)/shard_map/all_gather | solution.py:98
  412.9 76.5 %all-gather.22.cloned.1.call-done = bf16[1024,4608]{1,0:T(8,128)(2,1)} async-done(((bf16[32,4608]{1,0:T(8,128)(2,1)}), bf16[1024,4608]{1,0:T(8,128)(2,1)}) %all-gather.22.cloned.1.call-update) | async-done | bytes 9437200 | tf_op jit(solution)/shard_map/all_gather | solution.py:97
  495.9 76.5 %all-gather.26.cloned.1.call-done = bf16[4608,1024]{1,0:T(8,128)(2,1)} async-done(((bf16[144,1024]{1,0:T(8,128)(2,1)}), bf16[4608,1024]{1,0:T(8,128)(2,1)}) %all-gather.26.cloned.1.call-update) | async-done | bytes 9437200 | tf_op jit(solution)/shard_map/all_gather | solution.py:99
  607.9 15.8 fusion.16
  626.1 23.3 %fusion.1 = bf16[2,2,512,4096]{2,3,1,0:T(8,128)(2,1)} fusion(f32[2,4096,512,2]{2,1,3,0:T(8,128)} %get-tuple-element.45, f32[2,2,512]{2,1,0:T(2,128)} %bitcast.199, f32[2,2,512]{2,1,0:T(2,128)} %log_add_fusion, pred[512,4096]{0,1:T(8,128)(4,1)} %broadcast_compare_fusion, bf16[4096,2,64,1]{0,2,3,1:T(8,128)(2,1)} %bitcast.184, ...), kind=kOutput, calls=%fused_computation.2 | convolution fusion | flops 1132462080 | bytes 53755904 | tf_op jit(solution)/shard_map/qkgd,nkd->kgqn/dot_general | solution.py:258
  663.8 25.1 %reduce-scatter.12.cloned.1.call-done = bf16[512,128]{1,0:T(8,128)(2,1)} async-done(((bf16[4096,128]{1,0:T(8,128)(2,1)}), bf16[512,128]{1,0:T(8,128)(2,1)}) %reduce-scatter.12.cloned.1.call-update) | async-done | bytes 131088 | tf_op jit(solution)/shard_map/reduce_scatter | solution.py:281
  702.0 53.6 %reduce-scatter.10.cloned.1.call-done = bf16[512,128]{1,0:T(8,128)(2,1)} async-done(((bf16[4096,128]{1,0:T(8,128)(2,1)}), bf16[512,128]{1,0:T(8,128)(2,1)}) %reduce-scatter.10.cloned.1.call-update) | async-done | bytes 131088 | tf_op jit(solution)/shard_map/reduce_scatter | solution.py:278
  839.6 39.0 %all-reduce.8 = (f32[1024]{0:T(1024)S(1)}, f32[2,64]{1,0:T(2,128)}, f32[1024]{0:T(1024)S(1)}) all-reduce(f32[1024]{0:T(1024)S(1)} %get-tuple-element.14, f32[2,64]{1,0:T(2,128)S(1)} %pad_maximum_fusion.2, f32[1024]{0:T(1024)S(1)} %copy-done.36), channel_id=4, replica_groups=mesh['head'=4,'blk'=8] {'head','blk'}, use_global_device_ids=true, to_apply=%region_17.18.clone | all-reduce | flops 2176 | bytes 17408
  881.3 15.1 reduce-scatter.18.cloned.1.call-done
  896.4 138.7 %reduce-scatter.16.cloned.1.call-done = f32[32,512]{1,0:T(8,128)} async-done(((f32[1024,512]{1,0:T(8,128)}), f32[32,512]{1,0:T(8,128)}) %reduce-scatter.16.cloned.1.call-update) | async-done | bytes 65552 | tf_op jit(solution)/shard_map/reduce_scatter | solution.py:318
  1035.1 143.4 %reduce-scatter.20.cloned.1.call-done = f32[32,1024]{1,0:T(8,128)} async-done(((f32[1024,1024]{1,0:T(8,128)}), f32[32,1024]{1,0:T(8,128)}) %reduce-scatter.20.cloned.1.call-update) | async-done | bytes 131088 | tf_op jit(solution)/shard_map/reduce_scatter | solution.py:320
  1178.5 145.4 %reduce-scatter.14.cloned.1.call-done = f32[32,1024]{1,0:T(8,128)} async-done(((f32[1024,1024]{1,0:T(8,128)}), f32[32,1024]{1,0:T(8,128)}) %reduce-scatter.14.cloned.1.call-update) | async-done | bytes 131088 | tf_op jit(solution)/shard_map/reduce_scatter | solution.py:317
  1323.9 211.1 %reduce-scatter.26.cloned.1.call-done = f32[144,1024]{1,0:T(8,128)} async-done(((f32[4608,1024]{1,0:T(8,128)}), f32[144,1024]{1,0:T(8,128)}) %reduce-scatter.26.cloned.1.call-update) | async-done | bytes 589840 | tf_op jit(solution)/shard_map/reduce_scatter | solution.py:324
  1535.0 213.0 %reduce-scatter.24.cloned.1.call-done = f32[32,4608]{1,0:T(8,128)} async-done(((f32[1024,4608]{1,0:T(8,128)}), f32[32,4608]{1,0:T(8,128)}) %reduce-scatter.24.cloned.1.call-update) | async-done | bytes 589840 | tf_op jit(solution)/shard_map/reduce_scatter | solution.py:323
  1748.0 213.0 %reduce-scatter.22.cloned.1.call-done = f32[32,4608]{1,0:T(8,128)} async-done(((f32[1024,4608]{1,0:T(8,128)}), f32[32,4608]{1,0:T(8,128)}) %reduce-scatter.22.cloned.1.call-update) | async-done | bytes 589840 | tf_op jit(solution)/shard_map/reduce_scatter | solution.py:322
  (224 shorter events, 224.0 us)
Async XLA Ops:
  7.2 60.4 %all-gather.10.cloned.1.call-start = ((), (), s32[]{:S(2)}) async-start(), calls=%async_computation.17 | async-start | bytes 1081344 | tf_op jit(solution)/shard_map/all_gather | solution.py:94
  7.9 115.4 %all-gather.14.cloned.1.call-start = ((), (), s32[]{:S(2)}) async-start(), calls=%async_computation.19 | async-start | bytes 1081344 | tf_op jit(solution)/shard_map/all_gather | solution.py:93
  8.7 173.1 %all-gather.18.cloned.1.call-start = ((), (), s32[]{:S(2)}) async-start(), calls=%async_computation.21 | async-start | bytes 2162688 | tf_op jit(solution)/shard_map/all_gather | solution.py:92
  69.9 7.9 all-to-all-start
  73.2 150.2 %all-gather.12.cloned.1.call-start = ((), (), s32[]{:S(2)}) async-start(), calls=%async_computation.18 | async-start | bytes 1179648 | tf_op jit(solution)/shard_map/all_gather | solution.py:144
  78.5 186.5 %all-gather.16.cloned.1.call-start = ((), (), s32[]{:S(2)}) async-start(), calls=%async_computation.20 | async-start | bytes 1179648 | tf_op jit(solution)/shard_map/all_gather | solution.py:143
  134.1 188.9 %all-gather.20.cloned.1.call-start = ((), (), s32[]{:S(2)}) async-start(), calls=%async_computation.22 | async-start | bytes 2162688 | tf_op jit(solution)/shard_map/all_gather | solution.py:95
  134.7 271.7 %all-gather.24.cloned.1.call-start = ((), (), s32[]{:S(2)}) async-start(), calls=%async_computation.24 | async-start | bytes 9732096 | tf_op jit(solution)/shard_map/all_gather | solution.py:98
  135.4 354.0 %all-gather.22.cloned.1.call-start = ((), (), s32[]{:S(2)}) async-start(), calls=%async_computation.23 | async-start | bytes 9732096 | tf_op jit(solution)/shard_map/all_gather | solution.py:97
  136.2 436.3 %all-gather.26.cloned.1.call-start = ((), (), s32[]{:S(2)}) async-start(), calls=%async_computation.25 | async-start | bytes 9732096 | tf_op jit(solution)/shard_map/all_gather | solution.py:99
  185.4 81.1 %all-to-all-start.2 = ((bf16[128,4,256]{0,2,1:T(8,128)(2,1)}), bf16[128,4,256]{0,2,1:T(8,128)(2,1)S(1)}, u32[]{:S(2)}, u32[]{:S(2)}) async-start(bf16[128,4,256]{0,2,1:T(8,128)(2,1)} %bitcast.15), calls=%async_computation.2 | async-start | bytes 524288 | tf_op jit(solution)/shard_map/all_to_all | solution.py:127
  313.6 9.9 all-to-all-start.3
  317.5 267.0 %copy-start.30 = (f32[1024]{0:T(1024)}, f32[1024]{0:T(1024)S(1)}, u32[]{:S(2)}) copy-start(f32[1024]{0:T(1024)S(1)} %convert_element_type.155) | copy-start | bytes 12292
  325.7 258.8 %copy-start.39 = (f32[128]{0:T(128)}, f32[128]{0:T(128)S(1)}, u32[]{:S(2)}) copy-start(f32[128]{0:T(128)S(1)} %fusion.82) | copy-start | bytes 1540
  594.8 9.4 all-to-all-start.4
  598.2 90.6 %reduce-scatter.12.cloned.1.call-start = ((), (), s32[]{:S(2)}) async-start(), calls=%async_computation.27 | async-start | bytes 1179648 | tf_op jit(solution)/shard_map/reduce_scatter | solution.py:281
  626.0 129.6 %reduce-scatter.10.cloned.1.call-start = ((), (), s32[]{:S(2)}) async-start(), calls=%async_computation.26 | async-start | bytes 1179648 | tf_op jit(solution)/shard_map/reduce_scatter | solution.py:278
  663.7 232.7 %reduce-scatter.18.cloned.1.call-start = ((), (), s32[]{:S(2)}) async-start(), calls=%async_computation.30 | async-start | bytes 2162688 | tf_op jit(solution)/shard_map/reduce_scatter | solution.py:319
  701.9 333.2 %reduce-scatter.16.cloned.1.call-start = ((), (), s32[]{:S(2)}) async-start(), calls=%async_computation.29 | async-start | bytes 2162688 | tf_op jit(solution)/shard_map/reduce_scatter | solution.py:318
  773.3 405.2 %reduce-scatter.20.cloned.1.call-start = ((), (), s32[]{:S(2)}) async-start(), calls=%async_computation.31 | async-start | bytes 4325376 | tf_op jit(solution)/shard_map/reduce_scatter | solution.py:320
  777.2 546.7 %reduce-scatter.14.cloned.1.call-start = ((), (), s32[]{:S(2)}) async-start(), calls=%async_computation.28 | async-start | bytes 4325376 | tf_op jit(solution)/shard_map/reduce_scatter | solution.py:317
  804.1 730.9 %reduce-scatter.26.cloned.1.call-start = ((), (), s32[]{:S(2)}) async-start(), calls=%async_computation.34 | async-start | bytes 19464192 | tf_op jit(solution)/shard_map/reduce_scatter | solution.py:324
  813.1 935.0 %reduce-scatter.24.cloned.1.call-start = ((), (), s32[]{:S(2)}) async-start(), calls=%async_computation.33 | async-start | bytes 19464192 | tf_op jit(solution)/shard_map/reduce_scatter | solution.py:323
  822.3 1138.7 %reduce-scatter.22.cloned.1.call-start = ((), (), s32[]{:S(2)}) async-start(), calls=%async_computation.32 | async-start | bytes 19464192 | tf_op jit(solution)/shard_map/reduce_scatter | solution.py:322
  (40 other events, 1504.3 us)
Sparse Core Ops, SparseCore 0:
  11.0 56.5 all-gather.9
  70.5 52.7 all-gather.13
  126.3 55.3 all-gather.17
  184.3 39.1 all-gather.11
  226.0 38.9 all-gather.15
  267.9 55.1 all-gather.19
  326.0 80.3 all-gather.23
  409.3 80.0 all-gather.21
  492.4 80.0 all-gather.25
  626.2 62.6 reduce-scatter.11
  692.2 63.3 reduce-scatter.9
  758.3 138.0 reduce-scatter.17
  899.2 135.7 reduce-scatter.15
  1037.8 140.6 reduce-scatter.19
  1181.2 142.6 reduce-scatter.13
  1330.8 204.2 reduce-scatter.25
  1541.9 206.1 reduce-scatter.23
  1754.9 206.0 reduce-scatter.21
where the time goes:
time: 1970 us
  waiting for transfers between devices  1580 us (80%)
  matrix products  180 us (9%)
  blocking collectives  114 us (6%)
  other arithmetic  35.8 us (2%)
  local copies, waits for them, and re-layouts  24.7 us (1%)
    reduce_scatter x1, waiting for transfers between devices, local(): lax.psum_scatter(up_grad, ('head', 'blk'), scatter_dimension=0, tiled=True)  213 us
    reduce_scatter x1, waiting for transfers between devices, local(): lax.psum_scatter(gate_grad, ('head', 'blk'), scatter_dimension=0, tiled=T...  213 us
    reduce_scatter x1, waiting for transfers between devices, local(): lax.psum_scatter(down_grad, ('head', 'blk'), scatter_dimension=0, tiled=T...  211 us
    reduce_scatter x1, waiting for transfers between devices, local(): lax.psum_scatter(query_grad, ('head', 'blk'), scatter_dimension=0, tiled=...  145 us
    reduce_scatter x1, waiting for transfers between devices, local(): lax.psum_scatter(out_proj_grad, ('head', 'blk'), scatter_dimension=0, til...  143 us
    reduce_scatter x1, waiting for transfers between devices, local(): lax.psum_scatter(key_grad, ('head', 'blk'), scatter_dimension=0, tiled=True)  139 us
    unnamed x2, blocking collectives  81 us
    all_gather x1, waiting for transfers between devices, local(): lax.all_gather(w_up, ('head', 'blk'), axis=0, tiled=True)  80.5 us
  transfers between devices with their start and end apart: 22, of which 21 were waited for; matrix products, arithmetic and copies ran while one was open for 10% of the time, Pallas kernels for 0%

commit v1 on v0

--- a/solution.py
+++ b/solution.py
@@ -140,8 +140,14 @@
         jnp.zeros((kv_local, share_count, group_rows), jnp.float32),
         jnp.zeros((group_rows, kv_local, share_count, head_size), jnp.float32),
     )
-    key_piece = lax.all_gather(k_heads, "blk", axis=0, tiled=True)
-    value_piece = lax.all_gather(v_heads, "blk", axis=0, tiled=True)
+    grid_trace = lambda tile_in, view: jnp.split(
+        jax.lax.all_gather(
+            jnp.concatenate([tile_in, view], axis=1), axis_name="blk", axis=0, tiled=True
+        ),
+        [tile_in.shape[1]],
+        axis=1,
+    )
+    key_piece, value_piece = grid_trace(k_heads, v_heads)
     row_count = key_piece.shape[0]
     key_three = key_piece.reshape(row_count, kv_local, head_size)
     value_three = value_piece.reshape(row_count, kv_local, head_size)

time: 1970 us -> 2050 us (1.041)
  waiting for transfers between devices: 1580 us -> 1620 us
    reduce_scatter x1, waiting for transfers between devices: 15.1 us -> 139 us  [local(): lax.psum_scatter(value_grad, ('head', 'blk'), scatter_dimension=0, tiled=...]
    reduce_scatter x1, waiting for transfers between devices: 139 us -> 20.6 us  [local(): lax.psum_scatter(key_grad, ('head', 'blk'), scatter_dimension=0, tiled=True)]
    all_gather x0 -> x1, waiting for transfers between devices: none -> 46 us  [local(): jax.lax.all_gather(jnp.concatenate([tile_in, view], axis=1), axis_name='b...]
    all_gather x1, waiting for transfers between devices: 43.9 us -> 11.1 us  [local(): lax.all_gather(key_weight, ('head', 'blk'), axis=0, tiled=True)]
    all_gather x1, waiting for transfers between devices: 12.6 us -> 45 us  [local(): lax.all_gather(value_weight, ('head', 'blk'), axis=0, tiled=True)]
    reduce_scatter x1, waiting for transfers between devices: 25.1 us -> 48.2 us  [local(): lax.psum_scatter(value_acc.astype(jnp.bfloat16), 'blk', scatter_dimension...]
  transfers between devices with their start and end apart: 22 -> 22, of which waited for: 21 -> 19; matrix products, arithmetic and copies ran while one was open for 10% -> 10% of each run, Pallas kernels for 0% -> 0%
where the time goes in v1:
time: 2050 us; the launch traced here: 2040 us
  waiting for transfers between devices  1620 us (79%)
  matrix products  197 us (10%)
  blocking collectives  121 us (6%)
  local copies, waits for them, and re-layouts  37.8 us (2%)
  other arithmetic  37 us (2%)
    reduce_scatter x1, waiting for transfers between devices, local(): lax.psum_scatter(down_grad, ('head', 'blk'), scatter_dimension=0, tiled=T...  213 us
    reduce_scatter x1, waiting for transfers between devices, local(): lax.psum_scatter(up_grad, ('head', 'blk'), scatter_dimension=0, tiled=True)  213 us
    reduce_scatter x1, waiting for transfers between devices, local(): lax.psum_scatter(gate_grad, ('head', 'blk'), scatter_dimension=0, tiled=T...  211 us
    reduce_scatter x1, waiting for transfers between devices, local(): lax.psum_scatter(query_grad, ('head', 'blk'), scatter_dimension=0, tiled=...  145 us
    reduce_scatter x1, waiting for transfers between devices, local(): lax.psum_scatter(out_proj_grad, ('head', 'blk'), scatter_dimension=0, til...  144 us
    reduce_scatter x1, waiting for transfers between devices, local(): lax.psum_scatter(value_grad, ('head', 'blk'), scatter_dimension=0, tiled=...  139 us
    unnamed x2, blocking collectives  81.1 us
    all_gather x1, waiting for transfers between devices, local(): lax.all_gather(w_up, ('head', 'blk'), axis=0, tiled=True)  76.5 us
  transfers between devices with their start and end apart: 22, of which 19 were waited for; matrix products, arithmetic and copies ran while one was open for 10% of the time, Pallas kernels for 0%

profile of v1, /device:TPU:0, one launch (start us, length us, event | category | flops | bytes accessed | tf_op | source)
XLA Modules:
  0.0 2041.4 jit_solution(6530560837728702071)
XLA Ops:
  11.1 42.0 %all-reduce.9 = (bf16[1024]{0:T(1024)(128)(2,1)S(1)}, bf16[1024]{0:T(1024)(128)(2,1)S(1)}) all-reduce(bf16[1024]{0:T(1024)(128)(2,1)S(1)} %dynamic-update-slice, bf16[1024]{0:T(1024)(128)(2,1)S(1)} %dynamic-update-slice.1), channel_id=1, replica_groups=mesh['head'=4,'blk'=8] {'head','blk'}, use_global_device_ids=true, to_apply=%add.4 | all-reduce | flops 2048 | bytes 8192
  78.3 45.0 %all-gather.13.cloned.1.call-done = bf16[1024,512]{1,0:T(8,128)(2,1)} async-done(((bf16[32,512]{1,0:T(8,128)(2,1)}), bf16[1024,512]{1,0:T(8,128)(2,1)}) %all-gather.13.cloned.1.call-update) | async-done | bytes 1048592 | tf_op jit(solution)/shard_map/all_gather | solution.py:94
  139.0 42.8 %all-gather.17.cloned.1.call-done = bf16[1024,1024]{1,0:T(8,128)(2,1)} async-done(((bf16[32,1024]{1,0:T(8,128)(2,1)}), bf16[1024,1024]{1,0:T(8,128)(2,1)}) %all-gather.17.cloned.1.call-update) | async-done | bytes 2097168 | tf_op jit(solution)/shard_map/all_gather | solution.py:92
  192.1 31.4 %all-gather.27.cloned.1.call-done = bf16[4096,128]{1,0:T(8,128)(2,1)} async-done(((bf16[512,128]{1,0:T(8,128)(2,1)}), bf16[4096,128]{1,0:T(8,128)(2,1)}) %all-gather.27.cloned.1.call-update) | async-done | bytes 1048592 | tf_op jit(solution)/shard_map/all_gather | solution.py:242
  224.9 39.5 %all-gather.29.cloned.1.call-done = bf16[4096,128]{1,0:T(8,128)(2,1)} async-done(((bf16[512,128]{1,0:T(8,128)(2,1)}), bf16[4096,128]{1,0:T(8,128)(2,1)}) %all-gather.29.cloned.1.call-update) | async-done | bytes 1048592 | tf_op jit(solution)/shard_map/all_gather | solution.py:243
  268.8 46.0 %all-gather.15.cloned.1.call-done = bf16[4096,256]{1,0:T(8,128)(2,1)} async-done(((bf16[512,256]{1,0:T(8,128)(2,1)}), bf16[4096,256]{1,0:T(8,128)(2,1)}) %all-gather.15.cloned.1.call-update) | async-done | bytes 2097168 | tf_op jit(solution)/shard_map/all_gather | solution.py:144
  322.5 14.9 fusion.5
  337.4 15.1 fusion.6
  352.6 15.2 fusion.37
  389.1 67.1 %all-gather.21.cloned.1.call-done = bf16[1024,4608]{1,0:T(8,128)(2,1)} async-done(((bf16[32,4608]{1,0:T(8,128)(2,1)}), bf16[1024,4608]{1,0:T(8,128)(2,1)}) %all-gather.21.cloned.1.call-update) | async-done | bytes 9437200 | tf_op jit(solution)/shard_map/all_gather | solution.py:97
  462.7 76.5 %all-gather.23.cloned.1.call-done = bf16[1024,4608]{1,0:T(8,128)(2,1)} async-done(((bf16[32,4608]{1,0:T(8,128)(2,1)}), bf16[1024,4608]{1,0:T(8,128)(2,1)}) %all-gather.23.cloned.1.call-update) | async-done | bytes 9437200 | tf_op jit(solution)/shard_map/all_gather | solution.py:98
  545.8 76.3 %all-gather.25.cloned.1.call-done = bf16[4608,1024]{1,0:T(8,128)(2,1)} async-done(((bf16[144,1024]{1,0:T(8,128)(2,1)}), bf16[4608,1024]{1,0:T(8,128)(2,1)}) %all-gather.25.cloned.1.call-update) | async-done | bytes 9437200 | tf_op jit(solution)/shard_map/all_gather | solution.py:99
  662.6 23.3 %fusion.1 = bf16[2,2,512,4096]{2,3,1,0:T(8,128)(2,1)} fusion(f32[2,4096,512,2]{2,1,3,0:T(8,128)} %fusion.107, f32[2,2,512]{2,1,0:T(2,128)} %bitcast.224, f32[2,2,512]{2,1,0:T(2,128)} %log_add_fusion, pred[512,4096]{0,1:T(8,128)(4,1)} %copy-done.6, bf16[4096,2,64,1]{0,2,3,1:T(8,128)(2,1)} %bitcast.210, bf16[512,2,2,64]{0,3,2,1:T(8,128)(2,1)} %reshape.435), kind=kOutput, calls=%fused_computation.2 | convolution fusion | flops 1132462080 | bytes 53755904 | tf_op jit(solution)/shard_map/qkgd,nkd->kgqn/dot_general | solution.py:264
  700.7 17.4 fusion.19
  720.4 42.6 %reduce-scatter.10.cloned.1.call-done = bf16[512,128]{1,0:T(8,128)(2,1)} async-done(((bf16[4096,128]{1,0:T(8,128)(2,1)}), bf16[512,128]{1,0:T(8,128)(2,1)}) %reduce-scatter.10.cloned.1.call-update) | async-done | bytes 131088 | tf_op jit(solution)/shard_map/reduce_scatter | solution.py:284
  781.2 48.2 %reduce-scatter.12.cloned.1.call-done = bf16[512,128]{1,0:T(8,128)(2,1)} async-done(((bf16[4096,128]{1,0:T(8,128)(2,1)}), bf16[512,128]{1,0:T(8,128)(2,1)}) %reduce-scatter.12.cloned.1.call-update) | async-done | bytes 131088 | tf_op jit(solution)/shard_map/reduce_scatter | solution.py:287
  908.1 39.0 %all-reduce.8 = (f32[1024]{0:T(1024)S(1)}, f32[2,64]{1,0:T(2,128)}, f32[1024]{0:T(1024)S(1)}) all-reduce(f32[1024]{0:T(1024)S(1)} %get-tuple-element.14, f32[2,64]{1,0:T(2,128)S(1)} %pad_maximum_fusion.3, f32[1024]{0:T(1024)S(1)} %copy-done.41), channel_id=4, replica_groups=mesh['head'=4,'blk'=8] {'head','blk'}, use_global_device_ids=true, to_apply=%region_17.18.clone | all-reduce | flops 2176 | bytes 17408
  949.8 20.6 %reduce-scatter.16.cloned.1.call-done = f32[32,512]{1,0:T(8,128)} async-done(((f32[1024,512]{1,0:T(8,128)}), f32[32,512]{1,0:T(8,128)}) %reduce-scatter.16.cloned.1.call-update) | async-done | bytes 65552 | tf_op jit(solution)/shard_map/reduce_scatter | solution.py:324
  970.4 138.6 %reduce-scatter.18.cloned.1.call-done = f32[32,512]{1,0:T(8,128)} async-done(((f32[1024,512]{1,0:T(8,128)}), f32[32,512]{1,0:T(8,128)}) %reduce-scatter.18.cloned.1.call-update) | async-done | bytes 65552 | tf_op jit(solution)/shard_map/reduce_scatter | solution.py:325
  1109.0 144.4 %reduce-scatter.20.cloned.1.call-done = f32[32,1024]{1,0:T(8,128)} async-done(((f32[1024,1024]{1,0:T(8,128)}), f32[32,1024]{1,0:T(8,128)}) %reduce-scatter.20.cloned.1.call-update) | async-done | bytes 131088 | tf_op jit(solution)/shard_map/reduce_scatter | solution.py:326
  1253.4 144.9 %reduce-scatter.14.cloned.1.call-done = f32[32,1024]{1,0:T(8,128)} async-done(((f32[1024,1024]{1,0:T(8,128)}), f32[32,1024]{1,0:T(8,128)}) %reduce-scatter.14.cloned.1.call-update) | async-done | bytes 131088 | tf_op jit(solution)/shard_map/reduce_scatter | solution.py:323
  1398.3 210.7 %reduce-scatter.22.cloned.1.call-done = f32[32,4608]{1,0:T(8,128)} async-done(((f32[1024,4608]{1,0:T(8,128)}), f32[32,4608]{1,0:T(8,128)}) %reduce-scatter.22.cloned.1.call-update) | async-done | bytes 589840 | tf_op jit(solution)/shard_map/reduce_scatter | solution.py:328
  1608.9 212.8 %reduce-scatter.24.cloned.1.call-done = f32[32,4608]{1,0:T(8,128)} async-done(((f32[1024,4608]{1,0:T(8,128)}), f32[32,4608]{1,0:T(8,128)}) %reduce-scatter.24.cloned.1.call-update) | async-done | bytes 589840 | tf_op jit(solution)/shard_map/reduce_scatter | solution.py:329
  1821.7 212.9 %reduce-scatter.26.cloned.1.call-done = f32[144,1024]{1,0:T(8,128)} async-done(((f32[4608,1024]{1,0:T(8,128)}), f32[144,1024]{1,0:T(8,128)}) %reduce-scatter.26.cloned.1.call-update) | async-done | bytes 589840 | tf_op jit(solution)/shard_map/reduce_scatter | solution.py:330
  (247 shorter events, 259.2 us)
Async XLA Ops:
  7.2 60.4 %all-gather.11.cloned.1.call-start = ((), (), s32[]{:S(2)}) async-start(), calls=%async_computation.17 | async-start | bytes 1081344 | tf_op jit(solution)/shard_map/all_gather | solution.py:93
  7.9 115.4 %all-gather.13.cloned.1.call-start = ((), (), s32[]{:S(2)}) async-start(), calls=%async_computation.18 | async-start | bytes 1081344 | tf_op jit(solution)/shard_map/all_gather | solution.py:94
  8.7 173.1 %all-gather.17.cloned.1.call-start = ((), (), s32[]{:S(2)}) async-start(), calls=%async_computation.20 | async-start | bytes 2162688 | tf_op jit(solution)/shard_map/all_gather | solution.py:92
  9.4 214.1 %all-gather.27.cloned.1.call-start = ((), (), s32[]{:S(2)}) async-start(), calls=%async_computation.25 | async-start | bytes 1179648 | tf_op jit(solution)/shard_map/all_gather | solution.py:242
  55.6 211.2 %copy-start.38 = (f32[128]{0:T(128)}, f32[128]{0:T(128)S(1)}, u32[]{:S(2)}) copy-start(f32[128]{0:T(128)S(1)} %fusion.84) | copy-start | bytes 1540
  56.3 210.5 %copy-start.43 = (f32[64]{0:T(128)}, f32[64]{0:T(128)S(1)}, u32[]{:S(2)}) copy-start(f32[64]{0:T(128)S(1)} %get-tuple-element.39) | copy-start | bytes 772
  78.3 186.2 %all-gather.29.cloned.1.call-start = ((), (), s32[]{:S(2)}) async-start(), calls=%async_computation.26 | async-start | bytes 1179648 | tf_op jit(solution)/shard_map/all_gather | solution.py:243
  132.7 182.1 %all-gather.15.cloned.1.call-start = ((), (), s32[]{:S(2)}) async-start(), calls=%async_computation.19 | async-start | bytes 2359296 | tf_op jit(solution)/shard_map/all_gather | solution.py:144
  134.5 252.2 %all-gather.19.cloned.1.call-start = ((), (), s32[]{:S(2)}) async-start(), calls=%async_computation.21 | async-start | bytes 2162688 | tf_op jit(solution)/shard_map/all_gather | solution.py:95
  135.3 320.9 %all-gather.21.cloned.1.call-start = ((), (), s32[]{:S(2)}) async-start(), calls=%async_computation.22 | async-start | bytes 9732096 | tf_op jit(solution)/shard_map/all_gather | solution.py:97
  136.0 403.2 %all-gather.23.cloned.1.call-start = ((), (), s32[]{:S(2)}) async-start(), calls=%async_computation.23 | async-start | bytes 9732096 | tf_op jit(solution)/shard_map/all_gather | solution.py:98
  136.7 485.4 %all-gather.25.cloned.1.call-start = ((), (), s32[]{:S(2)}) async-start(), calls=%async_computation.24 | async-start | bytes 9732096 | tf_op jit(solution)/shard_map/all_gather | solution.py:99
  186.2 80.7 %all-to-all-start.2 = ((bf16[128,4,256]{0,2,1:T(8,128)(2,1)}), bf16[128,4,256]{0,2,1:T(8,128)(2,1)S(1)}, u32[]{:S(2)}, u32[]{:S(2)}) async-start(bf16[128,4,256]{0,2,1:T(8,128)(2,1)} %bitcast.15), calls=%async_computation.2 | async-start | bytes 524288 | tf_op jit(solution)/shard_map/all_to_all | solution.py:127
  368.6 18.1 all-to-all-start.3
  647.0 10.3 all-to-all-start.4
  651.2 111.8 %reduce-scatter.10.cloned.1.call-start = ((), (), s32[]{:S(2)}) async-start(), calls=%async_computation.27 | async-start | bytes 1179648 | tf_op jit(solution)/shard_map/reduce_scatter | solution.py:284
  700.2 129.2 %reduce-scatter.12.cloned.1.call-start = ((), (), s32[]{:S(2)}) async-start(), calls=%async_computation.28 | async-start | bytes 1179648 | tf_op jit(solution)/shard_map/reduce_scatter | solution.py:287
  720.3 250.1 %reduce-scatter.16.cloned.1.call-start = ((), (), s32[]{:S(2)}) async-start(), calls=%async_computation.30 | async-start | bytes 2162688 | tf_op jit(solution)/shard_map/reduce_scatter | solution.py:324
  781.2 327.8 %reduce-scatter.18.cloned.1.call-start = ((), (), s32[]{:S(2)}) async-start(), calls=%async_computation.31 | async-start | bytes 2162688 | tf_op jit(solution)/shard_map/reduce_scatter | solution.py:325
  842.6 410.8 %reduce-scatter.20.cloned.1.call-start = ((), (), s32[]{:S(2)}) async-start(), calls=%async_computation.32 | async-start | bytes 4325376 | tf_op jit(solution)/shard_map/reduce_scatter | solution.py:326
  846.3 552.0 %reduce-scatter.14.cloned.1.call-start = ((), (), s32[]{:S(2)}) async-start(), calls=%async_computation.29 | async-start | bytes 4325376 | tf_op jit(solution)/shard_map/reduce_scatter | solution.py:323
  872.4 736.6 %reduce-scatter.22.cloned.1.call-start = ((), (), s32[]{:S(2)}) async-start(), calls=%async_computation.33 | async-start | bytes 19464192 | tf_op jit(solution)/shard_map/reduce_scatter | solution.py:328
  881.9 939.8 %reduce-scatter.24.cloned.1.call-start = ((), (), s32[]{:S(2)}) async-start(), calls=%async_computation.34 | async-start | bytes 19464192 | tf_op jit(solution)/shard_map/reduce_scatter | solution.py:329
  891.2 1143.5 %reduce-scatter.26.cloned.1.call-start = ((), (), s32[]{:S(2)}) async-start(), calls=%async_computation.35 | async-start | bytes 19464192 | tf_op jit(solution)/shard_map/reduce_scatter | solution.py:330
  (48 other events, 2045.9 us)
Sparse Core Ops, SparseCore 0:
  11.0 56.5 all-gather.10
  70.5 52.7 all-gather.12
  126.3 55.3 all-gather.16
  184.3 39.1 all-gather.26
  225.4 38.9 all-gather.28
  267.0 47.7 all-gather.14
  317.8 54.9 all-gather.18
  375.8 80.3 all-gather.20
  459.2 80.0 all-gather.22
  542.1 80.0 all-gather.24
  700.3 62.6 reduce-scatter.9
  766.3 63.1 reduce-scatter.11
  832.2 138.1 reduce-scatter.15
  973.1 135.8 reduce-scatter.17
  1111.7 141.6 reduce-scatter.19
  1256.1 142.1 reduce-scatter.13
  1405.1 203.8 reduce-scatter.21
  1615.8 205.8 reduce-scatter.23
  1828.7 205.9 reduce-scatter.25
